TPU v7x, 32 devices: a whole 2x2x4 slice. The times are simulated.
32 devices in a mesh: mem: 4 (over x, core), lat: 8 (over z, y).
Axes of the slice: x: 2, y: 2, z: 4, core: 2. Of those that a mesh axis runs over, the one named last changes fastest.
Arguments:
- perturbation: bfloat16 [64, 128, 2048], P('mem', 'lat'), may hold values from -6 to 6
- obs_cells: int32 [8, 2048], P('lat'), may hold values from 0 to 32767
- obs_count: int32 [8], P('lat'), may hold values from 682 to 2048, as said below
- innovation: float32 [8, 2048], P('lat'), may hold values from -8 to 8
- obs_scale: float32 [8, 2048], P('lat'), may hold values from 0.3 to 3
Outputs:
- control: float32 [64, 64, 1024], P('mem', 'lat')
- increment: float32 [128, 2048], P('lat', 'mem')
Inputs may be any that keep to these rules, and one draw needn't show every extreme that they name: `obs_count`: at most 2048 live slots in a band, and some band has exactly 2048.
All inputs are finite; a program needn't handle non-finite values.
Results may differ from a plain program's by a relative error of at most 0.00035.
Values sent between devices are 32-bit elements; how exact they have to be, the bound alone decides.
No kernel may reach another device: no remote copies, remote signals or barrier semaphores. Data moves between devices by JAX's collectives and lax.ppermute only.
A program may use at most 64 MiB of HBM per device.

v0:
```python
import jax
import jax.numpy as jnp
from jax import lax
from jax.sharding import PartitionSpec as P

HALO = 8
LSIG = 3
ITERS = 3


def padded_2(block, sides, width):
    for axis, dim in sides:
        count = lax.axis_size(axis)
        forward = [(i, i + 1) for i in range(count - 1)]
        backward = [(target, source) for source, target in forward]
        low = lax.ppermute(
            lax.slice_in_dim(block, block.shape[dim] - width, None, axis=dim), axis, forward
        )
        high = lax.ppermute(lax.slice_in_dim(block, 0, width, axis=dim), axis, backward)
        block = jnp.concatenate([low, block, high], axis=dim)
    return block


def lat_weights():
    offsets = jnp.arange(2 * HALO + 1).astype(jnp.float32) - HALO
    spread = HALO / 2.0
    return 0.5 * jnp.exp(-offsets * offsets / (2.0 * spread * spread))


def lon_weights(coarse_cols):
    columns = jnp.arange(coarse_cols)
    distance = jnp.abs(columns[:, None] - columns[None, :])
    distance = jnp.minimum(distance, coarse_cols - distance).astype(jnp.float32)
    return jnp.exp(-distance * distance / (2.0 * LSIG * LSIG))


def band_matrix(row_count, lat_taps):
    rows = jnp.arange(row_count)[:, None]
    columns = jnp.arange(row_count + 2 * HALO)[None, :]
    offset_grid = columns - rows
    matrix = jnp.zeros((row_count, row_count + 2 * HALO), jnp.float32)
    for offset in range(2 * HALO + 1):
        matrix = matrix + jnp.where(offset_grid == offset, lat_taps[offset], 0.0)
    return matrix


def widen_lon(coarse):
    odd_part = 0.5 * (coarse + jnp.roll(coarse, -1, axis=-1))
    return jnp.stack([coarse, odd_part], axis=-1).reshape(
        coarse.shape[:-1] + (2 * coarse.shape[-1],)
    )


def narrow_lon(fine):
    paired = fine.reshape(fine.shape[:-1] + (fine.shape[-1] // 2, 2))
    odd_part = paired[..., 1]
    return paired[..., 0] + 0.5 * odd_part + 0.5 * jnp.roll(odd_part, 1, axis=-1)


def on_device(perturbation, obs_cells, obs_count, innovation, obs_scale):
    mem_count = lax.axis_size("mem")
    local_members, fine_rows, lon_cells = perturbation.shape
    coarse_rows = fine_rows // 2
    coarse_cols = lon_cells // 2
    member_scale = (local_members * mem_count - 1) ** (-0.5)
    lat_taps = lat_weights()
    banded = band_matrix(coarse_rows, lat_taps)
    circulant = lon_weights(coarse_cols)
    obs_index = obs_cells[0]
    row_index = obs_index // lon_cells
    col_index = obs_index % lon_cells
    active = jnp.arange(obs_index.shape[0]) < obs_count[0]
    is_first = lax.axis_index("mem") == 0
    target = innovation[0]
    saturation = obs_scale[0]

    def smooth(coarse):
        padded = padded_2(coarse, (("lat", 1),), HALO)
        return jnp.einsum(
            "ij,mjk->mik",
            banded,
            padded,
            precision=lax.Precision.HIGHEST,
            preferred_element_type=jnp.float32,
        )

    bend_mask = active & is_first
    increment = jnp.zeros((fine_rows, lon_cells), jnp.float32)
    control = jnp.zeros((local_members, coarse_rows, coarse_cols), jnp.float32)
    observed = jnp.zeros(obs_index.shape, jnp.float32)
    for iteration in range(ITERS):
        misfit = target - observed
        bounded = jnp.tanh(misfit / saturation)
        pull = jnp.where(active, saturation * bounded, 0.0)
        weight = jnp.where(bend_mask, 1.0 - bounded * bounded, 0.0)
        obs_field = (
            jnp.zeros((fine_rows * lon_cells,), jnp.float32)
            .at[obs_index]
            .add(pull)
            .reshape(fine_rows, lon_cells)
        )
        weighted = perturbation.astype(jnp.float32) * obs_field[None] * member_scale
        folded = narrow_lon(weighted.reshape(local_members, coarse_rows, 2, lon_cells).sum(axis=2))
        gradient = control - smooth(
            jnp.dot(
                folded,
                circulant,
                precision=lax.Precision.HIGHEST,
                preferred_element_type=jnp.float32,
            )
        )
        local_norm = jnp.sum(gradient * gradient)
        grad_norm = lax.psum(local_norm, ("mem", "lat"))
        direction = -gradient
        smoothed = smooth(direction)
        along = jnp.dot(
            smoothed, circulant, precision=lax.Precision.HIGHEST, preferred_element_type=jnp.float32
        )
        fine_block = jnp.repeat(widen_lon(along), 2, axis=1)
        partial_image = (
            jnp.sum(perturbation.astype(jnp.float32) * fine_block, axis=0) * member_scale
        )
        hits = lax.psum(partial_image[row_index, col_index], "mem")
        local_bend = jnp.sum(weight * hits * hits)
        bending = lax.psum(local_bend, ("mem", "lat"))
        step_size = grad_norm / (grad_norm + bending + 1e-06)
        control = control + step_size * direction
        increment = increment + step_size * partial_image
        observed = observed + step_size * hits
    increment = lax.psum_scatter(increment, "mem", scatter_dimension=1, tiled=True)
    return (control, increment)


def solution(mesh):
    in_specs = (P("mem", "lat", None), P("lat", None), P("lat"), P("lat", None), P("lat", None))
    out_specs = (P("mem", "lat", None), P("lat", "mem"))
    return jax.shard_map(
        on_device, mesh=mesh, in_specs=in_specs, out_specs=out_specs, check_vma=False
    )
```

profile of v0, /device:TPU:0, one launch (start us, length us, event | category | flops | bytes accessed | tf_op | source)
XLA Modules:
  0.0 612.5 jit_solution(4146181760270412733)
XLA Ops:
  9.4 11.3 %scatter_custom_fusion = f32[32768]{0:T(1024)S(1)} fusion(s32[2048]{0:T(1024)S(1)} %bitcast.168, f32[2048]{0:T(1024)S(1)} %multiply_select_fusion.2, f32[]{:T(128)} %constant.31.clone.1), kind=kCustom, calls=%fused_computation.133 | custom fusion | flops 2048 | bytes 131076 | tf_op jit(solution)/shard_map/scatter-add | solution.py:99
  33.6 7.2 %fusion.188 = (f32[16,8,1024,1]{0,1,3,2:T(8,128)}, f32[16,8,1024,1]{0,1,3,2:T(8,128)}) fusion(f32[16,8,1024,2]{0,1,3,2:T(8,128)} %bitcast.146), kind=kLoop, calls=%fused_computation.221 | loop fusion | bytes 2097152 | tf_op jit(solution)/shard_map/slice | solution.py:57
  50.9 4.9 collective-permute-start
  58.1 10.6 %select_add_fusion = f32[8,24]{1,0:T(8,128)S(1)} fusion(f32[]{:T(128)} %bitcast.25, f32[]{:T(128)} %bitcast.24, f32[]{:T(128)} %bitcast.23, f32[]{:T(128)} %bitcast.22, f32[]{:T(128)} %bitcast.21, f32[]{:T(128)} %bitcast.20, f32[]{:T(128)} %bitcast.19, f32[]{:T(128)} %bitcast.18, f32[]{:T(128)} %bitcast.17, f32[]{:T(128)} %bitcast.16, f32[]{:T(128)} %bitcast.15, ...), kind=kLoop, calls=%fused_computation.169 | loop fusion | flops 9792 | bytes 836 | tf_op jit(solution)/shard_map/add | solution.py:43
  68.7 9.5 %collective-permute-done = f32[16,8,1024]{2,1,0:T(8,128)S(1)} collective-permute-done((f32[16,8,1024]{2,1,0:T(8,128)S(1)}, f32[16,8,1024]{2,1,0:T(8,128)S(1)}, u32[]{:S(2)}, u32[]{:S(2)}) %collective-permute-start) | collective-permute-done | bytes 524320 | tf_op jit(solution)/shard_map/ppermute | solution.py:16
  85.6 20.2 %collective-permute-done.2 = f32[16,8,1024]{2,1,0:T(8,128)S(1)} collective-permute-done((f32[16,8,1024]{2,1,0:T(8,128)S(1)}, f32[16,8,1024]{2,1,0:T(8,128)S(1)}, u32[]{:S(2)}, u32[]{:S(2)}) %collective-permute-start.2) | collective-permute-done | bytes 524320 | tf_op jit(solution)/shard_map/ppermute | solution.py:16
  111.1 6.2 %copy.22 = f32[16,8,1024,2]{0,1,3,2:T(8,128)} copy(f32[16,8,1024,2]{2,1,0,3:T(8,128)S(1)} %pad_maximum_fusion) | data formatting | bytes 2097152 | tf_op jit(solution)/shard_map/stack | solution.py:49
  117.3 5.4 copy.23
  130.8 16.6 %gather_fusion = f32[2048]{0:T(1024)S(1)} fusion(f32[16,2048]{1,0:T(8,128)S(1)} %broadcast_multiply_fusion.2, s32[2048]{0:T(1024)S(1)} %bitcast.140), kind=kCustom, calls=%fused_computation | custom fusion | bytes 32768 | tf_op jit(solution)/shard_map/gather | solution.py:123
  147.4 5.8 psum.64
  153.8 45.1 %all-reduce.2 = (f32[]{:T(128)}, f32[]{:T(128)}) all-reduce(f32[]{:T(128)} %get-tuple-element.20, f32[]{:T(128)} %fusion.124), channel_id=1, replica_groups=mesh['mem'=4,'lat'=8] {'mem','lat'}, use_global_device_ids=true, to_apply=%region_3.4 | all-reduce | flops 2 | bytes 16 | tf_op jit(solution)/shard_map/psum | solution.py:113
  200.9 11.3 %scatter_custom_fusion.1 = f32[32768]{0:T(1024)S(1)} fusion(s32[2048]{0:T(1024)S(1)} %bitcast.169, f32[2048]{0:T(1024)S(1)} %multiply_select_fusion.1, f32[]{:T(128)} %constant.31.clone.1), kind=kCustom, calls=%fused_computation.131 | custom fusion | flops 2048 | bytes 131076 | tf_op jit(solution)/shard_map/scatter-add | solution.py:99
  221.6 4.8 copy.24
  226.4 7.2 %fusion.187 = (f32[16,8,1024,1]{0,1,3,2:T(8,128)}, f32[16,8,1024,1]{0,1,3,2:T(8,128)}) fusion(f32[16,8,1024,2]{0,1,3,2:T(8,128)} %bitcast.147), kind=kLoop, calls=%fused_computation.220 | loop fusion | bytes 2097152 | tf_op jit(solution)/shard_map/slice | solution.py:57
  249.7 19.2 %collective-permute-done.4 = f32[16,8,1024]{2,1,0:T(8,128)S(1)} collective-permute-done((f32[16,8,1024]{2,1,0:T(8,128)S(1)}, f32[16,8,1024]{2,1,0:T(8,128)S(1)}, u32[]{:S(2)}, u32[]{:S(2)}) %collective-permute-start.4) | collective-permute-done | bytes 524320 | tf_op jit(solution)/shard_map/ppermute | solution.py:16
  276.1 18.5 %collective-permute-done.6 = f32[16,8,1024]{2,1,0:T(8,128)S(1)} collective-permute-done((f32[16,8,1024]{2,1,0:T(8,128)S(1)}, f32[16,8,1024]{2,1,0:T(8,128)S(1)}, u32[]{:S(2)}, u32[]{:S(2)}) %collective-permute-start.6) | collective-permute-done | bytes 524320 | tf_op jit(solution)/shard_map/ppermute | solution.py:16
  299.9 6.2 %copy.27 = f32[16,8,1024,2]{0,1,3,2:T(8,128)} copy(f32[16,8,1024,2]{2,1,0,3:T(8,128)S(1)} %pad_maximum_fusion.1) | data formatting | bytes 2097152 | tf_op jit(solution)/shard_map/stack | solution.py:49
  306.1 5.4 copy.28
  319.6 16.6 %gather_fusion.1 = f32[2048]{0:T(1024)S(1)} fusion(f32[16,2048]{1,0:T(8,128)S(1)} %broadcast_multiply_fusion.1, s32[2048]{0:T(1024)S(1)} %bitcast.141), kind=kCustom, calls=%fused_computation.1 | custom fusion | bytes 32768 | tf_op jit(solution)/shard_map/gather | solution.py:123
  336.2 6.1 psum.67
  342.9 46.1 %all-reduce.1 = (f32[]{:T(128)}, f32[]{:T(128)}) all-reduce(f32[]{:T(128)} %get-tuple-element.18, f32[]{:T(128)} %fusion.125), channel_id=1, replica_groups=mesh['mem'=4,'lat'=8] {'mem','lat'}, use_global_device_ids=true, to_apply=%region_11.12 | all-reduce | flops 2 | bytes 16 | tf_op jit(solution)/shard_map/psum | solution.py:113
  391.7 11.4 %scatter_custom_fusion.2 = f32[32768]{0:T(1024)S(1)} fusion(s32[2048]{0:T(1024)} %bitcast.170, f32[2048]{0:T(1024)S(1)} %get-tuple-element.8, f32[]{:T(128)} %constant.31.clone.1), kind=kCustom, calls=%fused_computation.129 | custom fusion | flops 2048 | bytes 131584 | tf_op jit(solution)/shard_map/scatter-add | solution.py:99
  417.3 7.2 %fusion.186 = (f32[16,8,1024,1]{0,1,3,2:T(8,128)}, f32[16,8,1024,1]{0,1,3,2:T(8,128)}) fusion(f32[16,8,1024,2]{0,1,3,2:T(8,128)} %bitcast.148), kind=kLoop, calls=%fused_computation.219 | loop fusion | bytes 2097152 | tf_op jit(solution)/shard_map/slice | solution.py:57
  431.2 5.1 fusion.6
  442.3 19.2 %collective-permute-done.8 = f32[16,8,1024]{2,1,0:T(8,128)S(1)} collective-permute-done((f32[16,8,1024]{2,1,0:T(8,128)S(1)}, f32[16,8,1024]{2,1,0:T(8,128)S(1)}, u32[]{:S(2)}, u32[]{:S(2)}) %collective-permute-start.8) | collective-permute-done | bytes 524320 | tf_op jit(solution)/shard_map/ppermute | solution.py:16
  469.6 18.6 %collective-permute-done.10 = f32[16,8,1024]{2,1,0:T(8,128)S(1)} collective-permute-done((f32[16,8,1024]{2,1,0:T(8,128)S(1)}, f32[16,8,1024]{2,1,0:T(8,128)S(1)}, u32[]{:S(2)}, u32[]{:S(2)}) %collective-permute-start.10) | collective-permute-done | bytes 524320 | tf_op jit(solution)/shard_map/ppermute | solution.py:16
  494.7 6.2 %copy.32 = f32[16,8,1024,2]{0,1,3,2:T(8,128)} copy(f32[16,8,1024,2]{2,1,0,3:T(8,128)S(1)} %pad_maximum_fusion.2) | data formatting | bytes 2097152 | tf_op jit(solution)/shard_map/stack | solution.py:49
  500.9 5.4 copy.33
  514.4 16.6 %gather_fusion.2 = f32[2048]{0:T(1024)S(1)} fusion(f32[16,2048]{1,0:T(8,128)S(1)} %broadcast_multiply_fusion, s32[2048]{0:T(1024)S(1)} %bitcast.142), kind=kCustom, calls=%fused_computation.2 | custom fusion | bytes 32768 | tf_op jit(solution)/shard_map/gather | solution.py:123
  531.0 5.8 psum.70
  537.5 45.1 %all-reduce = (f32[]{:T(128)}, f32[]{:T(128)}) all-reduce(f32[]{:T(128)} %get-tuple-element.17, f32[]{:T(128)} %fusion.126), channel_id=1, replica_groups=mesh['mem'=4,'lat'=8] {'mem','lat'}, use_global_device_ids=true, to_apply=%region_19.20 | all-reduce | flops 2 | bytes 16 | tf_op jit(solution)/shard_map/psum | solution.py:113
  586.2 19.0 %reduce-scatter.2.cloned.1.call-done = f32[16,512]{1,0:T(8,128)} async-done(((f32[16,2048]{1,0:T(8,128)}), f32[16,512]{1,0:T(8,128)}) %reduce-scatter.2.cloned.1.call-update) | async-done | bytes 32784 | tf_op jit(solution)/shard_map/reduce_scatter | solution.py:130
  (111 shorter events, 147.0 us)
Async XLA Ops:
  7.2 598.1 %reduce-scatter.2.cloned.1.call-start = ((), (), s32[]{:S(2)}) async-start(), calls=%async_computation.1 | async-start | bytes 163840 | tf_op jit(solution)/shard_map/reduce_scatter | solution.py:130
  8.7 192.2 %copy-start.10 = (s32[2048,1]{0,1:T(1,128)}, s32[2048,1]{0,1:T(1,128)S(1)}, u32[]{:S(2)}) copy-start(s32[2048,1]{0,1:T(1,128)S(1)} %get-tuple-element.23) | copy-start | bytes 24580
  50.9 27.3 %collective-permute-start = (f32[16,8,1024]{2,1,0:T(8,128)S(1)}, f32[16,8,1024]{2,1,0:T(8,128)S(1)}, u32[]{:S(2)}, u32[]{:S(2)}) collective-permute-start(f32[16,8,1024]{2,1,0:T(8,128)S(1)} %fusion.14), channel_id=1, source_target_pairs={{0,1},{1,2},{2,3},{3,4},{4,5},{5,6},{6,7},{8,9},{9,10},{10,11},{11... | collective-permute-start | bytes 1572872 | tf_op jit(solution)/shard_map/ppermute | solution.py:16
  55.8 22.4 %collective-permute-start.1 = (f32[16,8,1024]{2,1,0:T(8,128)S(1)}, f32[16,8,1024]{2,1,0:T(8,128)S(1)}, u32[]{:S(2)}, u32[]{:S(2)}) collective-permute-start(f32[16,8,1024]{2,1,0:T(8,128)S(1)} %fusion.14), channel_id=1, source_target_pairs={{1,0},{2,1},{3,2},{4,3},{5,4},{6,5},{7,6},{9,8},{10,9},{11,10},{12... | collective-permute-start | bytes 1572872 | tf_op jit(solution)/shard_map/ppermute | solution.py:19
  68.7 225.9 %copy-start.7 = (f32[8,24]{1,0:T(8,128)}, f32[8,24]{1,0:T(8,128)S(1)}, u32[]{:S(2)}) copy-start(f32[8,24]{1,0:T(8,128)S(1)} %select_add_fusion) | copy-start | bytes 2308
  79.9 25.9 %collective-permute-start.2 = (f32[16,8,1024]{2,1,0:T(8,128)S(1)}, f32[16,8,1024]{2,1,0:T(8,128)S(1)}, u32[]{:S(2)}, u32[]{:S(2)}) collective-permute-start(f32[16,8,1024]{2,1,0:T(8,128)S(1)} %get-tuple-element.21), channel_id=1, source_target_pairs={{0,1},{1,2},{2,3},{3,4},{4,5},{5,6},{6,7},{8,9},{9,10},{10,11},{11... | collective-permute-start | bytes 1572872 | tf_op jit(solution)/shard_map/ppermute | solution.py:16
  84.3 21.5 %collective-permute-start.3 = (f32[16,8,1024]{2,1,0:T(8,128)S(1)}, f32[16,8,1024]{2,1,0:T(8,128)S(1)}, u32[]{:S(2)}, u32[]{:S(2)}) collective-permute-start(f32[16,8,1024]{2,1,0:T(8,128)S(1)} %get-tuple-element.21), channel_id=1, source_target_pairs={{1,0},{2,1},{3,2},{4,3},{5,4},{6,5},{7,6},{9,8},{10,9},{11,10},{12... | collective-permute-start | bytes 1572872 | tf_op jit(solution)/shard_map/ppermute | solution.py:19
  122.7 6.2 %copy-start = (bf16[16,16,2048]{2,1,0:T(8,128)(2,1)S(1)}, bf16[16,16,2048]{2,1,0:T(8,128)(2,1)}, u32[]{:S(2)}) copy-start(bf16[16,16,2048]{2,1,0:T(8,128)(2,1)} %param.5) | copy-start | bytes 3145732
  130.7 22.5 %copy-start.2 = (f32[1,2048]{1,0:T(1,128)S(1)}, f32[1,2048]{1,0:T(1,128)}, u32[]{:S(2)}) copy-start(f32[1,2048]{1,0:T(1,128)} %param.9) | copy-start | bytes 24580
  130.8 22.5 %copy-start.3 = (f32[1,2048]{1,0:T(1,128)S(1)}, f32[1,2048]{1,0:T(1,128)}, u32[]{:S(2)}) copy-start(f32[1,2048]{1,0:T(1,128)} %param.8) | copy-start | bytes 24580
  153.2 68.4 %copy-start.5 = (f32[2048]{0:T(1024)}, f32[2048]{0:T(1024)S(1)}, u32[]{:S(2)}) copy-start(f32[2048]{0:T(1024)S(1)} %psum.64) | copy-start | bytes 24580
  243.7 25.1 %collective-permute-start.4 = (f32[16,8,1024]{2,1,0:T(8,128)S(1)}, f32[16,8,1024]{2,1,0:T(8,128)S(1)}, u32[]{:S(2)}, u32[]{:S(2)}) collective-permute-start(f32[16,8,1024]{2,1,0:T(8,128)S(1)} %fusion.10), channel_id=1, source_target_pairs={{0,1},{1,2},{2,3},{3,4},{4,5},{5,6},{6,7},{8,9},{9,10},{10,11},{11... | collective-permute-start | bytes 1572872 | tf_op jit(solution)/shard_map/ppermute | solution.py:16
  248.2 20.6 %collective-permute-start.5 = (f32[16,8,1024]{2,1,0:T(8,128)S(1)}, f32[16,8,1024]{2,1,0:T(8,128)S(1)}, u32[]{:S(2)}, u32[]{:S(2)}) collective-permute-start(f32[16,8,1024]{2,1,0:T(8,128)S(1)} %fusion.10), channel_id=1, source_target_pairs={{1,0},{2,1},{3,2},{4,3},{5,4},{6,5},{7,6},{9,8},{10,9},{11,10},{12... | collective-permute-start | bytes 1572872 | tf_op jit(solution)/shard_map/ppermute | solution.py:19
  270.4 24.2 %collective-permute-start.6 = (f32[16,8,1024]{2,1,0:T(8,128)S(1)}, f32[16,8,1024]{2,1,0:T(8,128)S(1)}, u32[]{:S(2)}, u32[]{:S(2)}) collective-permute-start(f32[16,8,1024]{2,1,0:T(8,128)S(1)} %get-tuple-element.19), channel_id=1, source_target_pairs={{0,1},{1,2},{2,3},{3,4},{4,5},{5,6},{6,7},{8,9},{9,10},{10,11},{11... | collective-permute-start | bytes 1572872 | tf_op jit(solution)/shard_map/ppermute | solution.py:16
  274.8 19.8 %collective-permute-start.7 = (f32[16,8,1024]{2,1,0:T(8,128)S(1)}, f32[16,8,1024]{2,1,0:T(8,128)S(1)}, u32[]{:S(2)}, u32[]{:S(2)}) collective-permute-start(f32[16,8,1024]{2,1,0:T(8,128)S(1)} %get-tuple-element.19), channel_id=1, source_target_pairs={{1,0},{2,1},{3,2},{4,3},{5,4},{6,5},{7,6},{9,8},{10,9},{11,10},{12... | collective-permute-start | bytes 1572872 | tf_op jit(solution)/shard_map/ppermute | solution.py:19
  319.6 22.7 %copy-start.4 = (f32[1,2048]{1,0:T(1,128)S(1)}, f32[1,2048]{1,0:T(1,128)}, u32[]{:S(2)}) copy-start(f32[1,2048]{1,0:T(1,128)} %param.8) | copy-start | bytes 24580
  319.6 22.7 %copy-start.6 = (f32[2048]{0:T(1024)S(1)}, f32[2048]{0:T(1024)}, u32[]{:S(2)}) copy-start(f32[2048]{0:T(1024)} %copy-done.5) | copy-start | bytes 24580
  431.2 30.3 %copy-start.8 = (f32[8,24]{1,0:T(8,128)S(1)}, f32[8,24]{1,0:T(8,128)}, u32[]{:S(2)}) copy-start(f32[8,24]{1,0:T(8,128)} %copy-done.7) | copy-start | bytes 2308
  436.3 25.3 %collective-permute-start.8 = (f32[16,8,1024]{2,1,0:T(8,128)S(1)}, f32[16,8,1024]{2,1,0:T(8,128)S(1)}, u32[]{:S(2)}, u32[]{:S(2)}) collective-permute-start(f32[16,8,1024]{2,1,0:T(8,128)S(1)} %fusion.6), channel_id=1, source_target_pairs={{0,1},{1,2},{2,3},{3,4},{4,5},{5,6},{6,7},{8,9},{9,10},{10,11},{11... | collective-permute-start | bytes 1572872 | tf_op jit(solution)/shard_map/ppermute | solution.py:16
  440.8 20.8 %collective-permute-start.9 = (f32[16,8,1024]{2,1,0:T(8,128)S(1)}, f32[16,8,1024]{2,1,0:T(8,128)S(1)}, u32[]{:S(2)}, u32[]{:S(2)}) collective-permute-start(f32[16,8,1024]{2,1,0:T(8,128)S(1)} %fusion.6), channel_id=1, source_target_pairs={{1,0},{2,1},{3,2},{4,3},{5,4},{6,5},{7,6},{9,8},{10,9},{11,10},{12... | collective-permute-start | bytes 1572872 | tf_op jit(solution)/shard_map/ppermute | solution.py:19
  463.9 24.3 %collective-permute-start.10 = (f32[16,8,1024]{2,1,0:T(8,128)S(1)}, f32[16,8,1024]{2,1,0:T(8,128)S(1)}, u32[]{:S(2)}, u32[]{:S(2)}) collective-permute-start(f32[16,8,1024]{2,1,0:T(8,128)S(1)} %get-tuple-element.16), channel_id=1, source_target_pairs={{0,1},{1,2},{2,3},{3,4},{4,5},{5,6},{6,7},{8,9},{9,10},{10,11},{11... | collective-permute-start | bytes 1572872 | tf_op jit(solution)/shard_map/ppermute | solution.py:16
  468.3 19.9 %collective-permute-start.11 = (f32[16,8,1024]{2,1,0:T(8,128)S(1)}, f32[16,8,1024]{2,1,0:T(8,128)}, u32[]{:S(2)}, u32[]{:S(2)}) collective-permute-start(f32[16,8,1024]{2,1,0:T(8,128)S(1)} %get-tuple-element.16), channel_id=1, source_target_pairs={{1,0},{2,1},{3,2},{4,3},{5,4},{6,5},{7,6},{9,8},{10,9},{11,10},{12... | collective-permute-start | bytes 1572872 | tf_op jit(solution)/shard_map/ppermute | solution.py:19
  514.4 22.5 %copy-start.9 = (f32[2048]{0:T(1024)S(1)}, f32[2048]{0:T(1024)}, u32[]{:S(2)}) copy-start(f32[2048]{0:T(1024)} %get-tuple-element.9) | copy-start | bytes 24580
  514.4 70.9 %copy-start.1 = (f32[16,8,1024]{2,1,0:T(8,128)S(1)}, f32[16,8,1024]{2,1,0:T(8,128)}, u32[]{:S(2)}) copy-start(f32[16,8,1024]{2,1,0:T(8,128)} %get-tuple-element.42) | copy-start | bytes 1572868
Sparse Core Ops, SparseCore 0:
  585.4 19.8 reduce-scatter.1
where the time goes:
time: 622 us; the launch traced here: 613 us
  local copies, waits for them, and re-layouts  169 us (27%)
  blocking collectives  154 us (25%)
  waiting for transfers between devices  124 us (20%)
  other arithmetic  74.9 us (12%)
  starting transfers between devices  35.5 us (6%)
  matrix products  33.7 us (5%)
  between operations  21.7 us (3%)
    psum x3, blocking collectives, on_device(): grad_norm = lax.psum(local_norm, ('mem', 'lat'))  136 us
    ppermute x6, waiting for transfers between devices, padded_2(): lax.ppermute(lax.slice_in_dim(block, block.shape[dim] - width, None, axis...  105 us
    gather x3, local copies, waits for them, and re-layouts, on_device(): hits = lax.psum(partial_image[row_index, col_index], 'mem')  50 us
    scatter-add x3, other arithmetic, on_device(): obs_field = jnp.zeros((fine_rows * lon_cells,), jnp.float32).at[obs_index...  34 us
    ppermute x6, starting transfers between devices, padded_2(): lax.ppermute(lax.slice_in_dim(block, block.shape[dim] - width, None, axis...  27.1 us
    slice x3, local copies, waits for them, and re-layouts, narrow_lon(): paired[..., 0] + 0.5 * odd_part + 0.5 * jnp.roll(odd_part, 1, axis=-1)  21.6 us
    reduce_scatter x1, waiting for transfers between devices, on_device(): lax.psum_scatter(increment, 'mem', scatter_dimension=1, tiled=True)  19 us
    another operation x3, local copies, waits for them, and re-layouts, widen_lon(): jnp.stack([coarse, odd_part], axis=-1)  18.6 us
  transfers between devices with their start and end apart: 13, of which 7 were waited for; matrix products, arithmetic and copies ran while one was open for 2% of the time, Pallas kernels for 0%

commit v1 on v0

--- a/solution.py
+++ b/solution.py
@@ -120,7 +120,7 @@
         partial_image = (
             jnp.sum(perturbation.astype(jnp.float32) * fine_block, axis=0) * member_scale
         )
-        hits = lax.psum(partial_image[row_index, col_index], "mem")
+        hits = jnp.sum(lax.all_gather(partial_image[row_index, col_index], "mem"), axis=0)
         local_bend = jnp.sum(weight * hits * hits)
         bending = lax.psum(local_bend, ("mem", "lat"))
         step_size = grad_norm / (grad_norm + bending + 1e-06)

time: 622 us -> 620 us (level)
  blocking collectives: 154 us -> 146 us
    psum x3 -> x0, blocking collectives: 17.6 us -> none  [on_device(): hits = lax.psum(partial_image[row_index, col_index], 'mem')]
    all_gather x0 -> x3, blocking collectives: none -> 15.6 us  [on_device(): lax.all_gather(partial_image[row_index, col_index], 'mem')]
where the time goes in v1:
time: 620 us; the launch traced here: 610 us
  local copies, waits for them, and re-layouts  169 us (27%)
  blocking collectives  146 us (24%)
  waiting for transfers between devices  129 us (21%)
  other arithmetic  74.9 us (12%)
  starting transfers between devices  35.5 us (6%)
  matrix products  33.7 us (5%)
  between operations  21.7 us (4%)
    psum x3, blocking collectives, on_device(): grad_norm = lax.psum(local_norm, ('mem', 'lat'))  131 us
    ppermute x6, waiting for transfers between devices, padded_2(): lax.ppermute(lax.slice_in_dim(block, block.shape[dim] - width, None, axis...  109 us
    gather x3, local copies, waits for them, and re-layouts, on_device(): partial_image[row_index, col_index]  50 us
    scatter-add x3, other arithmetic, on_device(): obs_field = jnp.zeros((fine_rows * lon_cells,), jnp.float32).at[obs_index...  34 us
    ppermute x6, starting transfers between devices, padded_2(): lax.ppermute(lax.slice_in_dim(block, block.shape[dim] - width, None, axis...  27.1 us
    slice x3, local copies, waits for them, and re-layouts, narrow_lon(): paired[..., 0] + 0.5 * odd_part + 0.5 * jnp.roll(odd_part, 1, axis=-1)  21.6 us
    reduce_scatter x1, waiting for transfers between devices, on_device(): lax.psum_scatter(increment, 'mem', scatter_dimension=1, tiled=True)  20 us
    another operation x3, local copies, waits for them, and re-layouts, widen_lon(): jnp.stack([coarse, odd_part], axis=-1)  18.6 us
  transfers between devices with their start and end apart: 13, of which 7 were waited for; matrix products, arithmetic and copies ran while one was open for 2% of the time, Pallas kernels for 0%

profile of v1, /device:TPU:0, one launch (start us, length us, event | category | flops | bytes accessed | tf_op | source)
XLA Modules:
  0.0 610.1 jit_solution(13759581346806380157)
XLA Ops:
  9.4 11.3 %scatter_custom_fusion = f32[32768]{0:T(1024)S(1)} fusion(s32[2048]{0:T(1024)S(1)} %bitcast.168, f32[2048]{0:T(1024)S(1)} %multiply_select_fusion.2, f32[]{:T(128)} %constant.31.clone.1), kind=kCustom, calls=%fused_computation.133 | custom fusion | flops 2048 | bytes 131076 | tf_op jit(solution)/shard_map/scatter-add | solution.py:99
  28.8 4.8 copy.34
  33.6 7.2 %fusion.188 = (f32[16,8,1024,1]{0,1,3,2:T(8,128)}, f32[16,8,1024,1]{0,1,3,2:T(8,128)}) fusion(f32[16,8,1024,2]{0,1,3,2:T(8,128)} %bitcast.146), kind=kLoop, calls=%fused_computation.221 | loop fusion | bytes 2097152 | tf_op jit(solution)/shard_map/slice | solution.py:57
  50.9 4.9 collective-permute-start
  58.1 10.6 %select_add_fusion = f32[8,24]{1,0:T(8,128)S(1)} fusion(f32[]{:T(128)} %bitcast.25, f32[]{:T(128)} %bitcast.24, f32[]{:T(128)} %bitcast.23, f32[]{:T(128)} %bitcast.22, f32[]{:T(128)} %bitcast.21, f32[]{:T(128)} %bitcast.20, f32[]{:T(128)} %bitcast.19, f32[]{:T(128)} %bitcast.18, f32[]{:T(128)} %bitcast.17, f32[]{:T(128)} %bitcast.16, f32[]{:T(128)} %bitcast.15, ...), kind=kLoop, calls=%fused_computation.169 | loop fusion | flops 9792 | bytes 836 | tf_op jit(solution)/shard_map/add | solution.py:43
  68.7 9.5 %collective-permute-done = f32[16,8,1024]{2,1,0:T(8,128)S(1)} collective-permute-done((f32[16,8,1024]{2,1,0:T(8,128)S(1)}, f32[16,8,1024]{2,1,0:T(8,128)S(1)}, u32[]{:S(2)}, u32[]{:S(2)}) %collective-permute-start) | collective-permute-done | bytes 524320 | tf_op jit(solution)/shard_map/ppermute | solution.py:16
  85.6 20.2 %collective-permute-done.2 = f32[16,8,1024]{2,1,0:T(8,128)S(1)} collective-permute-done((f32[16,8,1024]{2,1,0:T(8,128)S(1)}, f32[16,8,1024]{2,1,0:T(8,128)S(1)}, u32[]{:S(2)}, u32[]{:S(2)}) %collective-permute-start.2) | collective-permute-done | bytes 524320 | tf_op jit(solution)/shard_map/ppermute | solution.py:16
  111.1 6.2 %copy.37 = f32[16,8,1024,2]{0,1,3,2:T(8,128)} copy(f32[16,8,1024,2]{2,1,0,3:T(8,128)S(1)} %pad_maximum_fusion) | data formatting | bytes 2097152 | tf_op jit(solution)/shard_map/stack | solution.py:49
  117.3 5.4 copy.38
  130.8 16.6 %gather_fusion = f32[2048]{0:T(1024)S(1)} fusion(f32[16,2048]{1,0:T(8,128)S(1)} %broadcast_multiply_fusion.2, s32[2048]{0:T(1024)S(1)} %bitcast.140), kind=kCustom, calls=%fused_computation | custom fusion | bytes 32768 | tf_op jit(solution)/shard_map/gather | solution.py:123
  147.4 5.2 all-gather
  153.3 43.9 %all-reduce.2 = (f32[]{:T(128)}, f32[]{:T(128)}) all-reduce(f32[]{:T(128)} %get-tuple-element.20, f32[]{:T(128)} %fusion.124), channel_id=1, replica_groups=mesh['mem'=4,'lat'=8] {'mem','lat'}, use_global_device_ids=true, to_apply=%region_3.4 | all-reduce | flops 2 | bytes 16 | tf_op jit(solution)/shard_map/psum | solution.py:113
  199.2 11.3 %scatter_custom_fusion.1 = f32[32768]{0:T(1024)S(1)} fusion(s32[2048]{0:T(1024)S(1)} %bitcast.169, f32[2048]{0:T(1024)S(1)} %multiply_select_fusion.1, f32[]{:T(128)} %constant.31.clone.1), kind=kCustom, calls=%fused_computation.131 | custom fusion | flops 2048 | bytes 131076 | tf_op jit(solution)/shard_map/scatter-add | solution.py:99
  224.7 7.2 %fusion.187 = (f32[16,8,1024,1]{0,1,3,2:T(8,128)}, f32[16,8,1024,1]{0,1,3,2:T(8,128)}) fusion(f32[16,8,1024,2]{0,1,3,2:T(8,128)} %bitcast.147), kind=kLoop, calls=%fused_computation.220 | loop fusion | bytes 2097152 | tf_op jit(solution)/shard_map/slice | solution.py:57
  247.9 20.1 %collective-permute-done.4 = f32[16,8,1024]{2,1,0:T(8,128)S(1)} collective-permute-done((f32[16,8,1024]{2,1,0:T(8,128)S(1)}, f32[16,8,1024]{2,1,0:T(8,128)S(1)}, u32[]{:S(2)}, u32[]{:S(2)}) %collective-permute-start.4) | collective-permute-done | bytes 524320 | tf_op jit(solution)/shard_map/ppermute | solution.py:16
  275.4 19.4 %collective-permute-done.6 = f32[16,8,1024]{2,1,0:T(8,128)S(1)} collective-permute-done((f32[16,8,1024]{2,1,0:T(8,128)S(1)}, f32[16,8,1024]{2,1,0:T(8,128)S(1)}, u32[]{:S(2)}, u32[]{:S(2)}) %collective-permute-start.6) | collective-permute-done | bytes 524320 | tf_op jit(solution)/shard_map/ppermute | solution.py:16
  300.1 6.2 %copy.42 = f32[16,8,1024,2]{0,1,3,2:T(8,128)} copy(f32[16,8,1024,2]{2,1,0,3:T(8,128)S(1)} %pad_maximum_fusion.1) | data formatting | bytes 2097152 | tf_op jit(solution)/shard_map/stack | solution.py:49
  306.3 5.4 copy.43
  319.8 16.6 %gather_fusion.1 = f32[2048]{0:T(1024)S(1)} fusion(f32[16,2048]{1,0:T(8,128)S(1)} %broadcast_multiply_fusion.1, s32[2048]{0:T(1024)S(1)} %bitcast.141), kind=kCustom, calls=%fused_computation.1 | custom fusion | bytes 32768 | tf_op jit(solution)/shard_map/gather | solution.py:123
  336.4 5.2 all-gather.1
  342.3 44.0 %all-reduce.1 = (f32[]{:T(128)}, f32[]{:T(128)}) all-reduce(f32[]{:T(128)} %get-tuple-element.18, f32[]{:T(128)} %fusion.125), channel_id=1, replica_groups=mesh['mem'=4,'lat'=8] {'mem','lat'}, use_global_device_ids=true, to_apply=%region_11.12 | all-reduce | flops 2 | bytes 16 | tf_op jit(solution)/shard_map/psum | solution.py:113
  389.0 11.4 %scatter_custom_fusion.2 = f32[32768]{0:T(1024)S(1)} fusion(s32[2048]{0:T(1024)} %bitcast.170, f32[2048]{0:T(1024)S(1)} %get-tuple-element.8, f32[]{:T(128)} %constant.31.clone.1), kind=kCustom, calls=%fused_computation.129 | custom fusion | flops 2048 | bytes 131584 | tf_op jit(solution)/shard_map/scatter-add | solution.py:99
  414.6 7.2 %fusion.186 = (f32[16,8,1024,1]{0,1,3,2:T(8,128)}, f32[16,8,1024,1]{0,1,3,2:T(8,128)}) fusion(f32[16,8,1024,2]{0,1,3,2:T(8,128)} %bitcast.148), kind=kLoop, calls=%fused_computation.219 | loop fusion | bytes 2097152 | tf_op jit(solution)/shard_map/slice | solution.py:57
  428.5 5.1 fusion.6
  439.6 20.2 %collective-permute-done.8 = f32[16,8,1024]{2,1,0:T(8,128)S(1)} collective-permute-done((f32[16,8,1024]{2,1,0:T(8,128)S(1)}, f32[16,8,1024]{2,1,0:T(8,128)S(1)}, u32[]{:S(2)}, u32[]{:S(2)}) %collective-permute-start.8) | collective-permute-done | bytes 524320 | tf_op jit(solution)/shard_map/ppermute | solution.py:16
  467.9 19.6 %collective-permute-done.10 = f32[16,8,1024]{2,1,0:T(8,128)S(1)} collective-permute-done((f32[16,8,1024]{2,1,0:T(8,128)S(1)}, f32[16,8,1024]{2,1,0:T(8,128)S(1)}, u32[]{:S(2)}, u32[]{:S(2)}) %collective-permute-start.10) | collective-permute-done | bytes 524320 | tf_op jit(solution)/shard_map/ppermute | solution.py:16
  494.0 6.2 %copy.47 = f32[16,8,1024,2]{0,1,3,2:T(8,128)} copy(f32[16,8,1024,2]{2,1,0,3:T(8,128)S(1)} %pad_maximum_fusion.2) | data formatting | bytes 2097152 | tf_op jit(solution)/shard_map/stack | solution.py:49
  500.2 5.4 copy.48
  513.7 16.6 %gather_fusion.2 = f32[2048]{0:T(1024)S(1)} fusion(f32[16,2048]{1,0:T(8,128)S(1)} %broadcast_multiply_fusion, s32[2048]{0:T(1024)S(1)} %bitcast.142), kind=kCustom, calls=%fused_computation.2 | custom fusion | bytes 32768 | tf_op jit(solution)/shard_map/gather | solution.py:123
  530.3 5.2 all-gather.2
  536.3 42.8 %all-reduce = (f32[]{:T(128)}, f32[]{:T(128)}) all-reduce(f32[]{:T(128)} %get-tuple-element.17, f32[]{:T(128)} %fusion.126), channel_id=1, replica_groups=mesh['mem'=4,'lat'=8] {'mem','lat'}, use_global_device_ids=true, to_apply=%region_19.20 | all-reduce | flops 2 | bytes 16 | tf_op jit(solution)/shard_map/psum | solution.py:113
  582.8 20.0 %reduce-scatter.2.cloned.1.call-done = f32[16,512]{1,0:T(8,128)} async-done(((f32[16,2048]{1,0:T(8,128)}), f32[16,512]{1,0:T(8,128)}) %reduce-scatter.2.cloned.1.call-update) | async-done | bytes 32784 | tf_op jit(solution)/shard_map/reduce_scatter | solution.py:130
  (117 shorter events, 147.1 us)
Async XLA Ops:
  7.2 595.6 %reduce-scatter.2.cloned.1.call-start = ((), (), s32[]{:S(2)}) async-start(), calls=%async_computation.1 | async-start | bytes 163840 | tf_op jit(solution)/shard_map/reduce_scatter | solution.py:130
  8.7 190.5 %copy-start.10 = (s32[2048,1]{0,1:T(1,128)}, s32[2048,1]{0,1:T(1,128)S(1)}, u32[]{:S(2)}) copy-start(s32[2048,1]{0,1:T(1,128)S(1)} %get-tuple-element.23) | copy-start | bytes 24580
  50.9 27.3 %collective-permute-start = (f32[16,8,1024]{2,1,0:T(8,128)S(1)}, f32[16,8,1024]{2,1,0:T(8,128)S(1)}, u32[]{:S(2)}, u32[]{:S(2)}) collective-permute-start(f32[16,8,1024]{2,1,0:T(8,128)S(1)} %fusion.14), channel_id=1, source_target_pairs={{0,1},{1,2},{2,3},{3,4},{4,5},{5,6},{6,7},{8,9},{9,10},{10,11},{11... | collective-permute-start | bytes 1572872 | tf_op jit(solution)/shard_map/ppermute | solution.py:16
  55.8 22.4 %collective-permute-start.1 = (f32[16,8,1024]{2,1,0:T(8,128)S(1)}, f32[16,8,1024]{2,1,0:T(8,128)S(1)}, u32[]{:S(2)}, u32[]{:S(2)}) collective-permute-start(f32[16,8,1024]{2,1,0:T(8,128)S(1)} %fusion.14), channel_id=1, source_target_pairs={{1,0},{2,1},{3,2},{4,3},{5,4},{6,5},{7,6},{9,8},{10,9},{11,10},{12... | collective-permute-start | bytes 1572872 | tf_op jit(solution)/shard_map/ppermute | solution.py:19
  68.7 226.1 %copy-start.7 = (f32[8,24]{1,0:T(8,128)}, f32[8,24]{1,0:T(8,128)S(1)}, u32[]{:S(2)}) copy-start(f32[8,24]{1,0:T(8,128)S(1)} %select_add_fusion) | copy-start | bytes 2308
  79.9 25.9 %collective-permute-start.2 = (f32[16,8,1024]{2,1,0:T(8,128)S(1)}, f32[16,8,1024]{2,1,0:T(8,128)S(1)}, u32[]{:S(2)}, u32[]{:S(2)}) collective-permute-start(f32[16,8,1024]{2,1,0:T(8,128)S(1)} %get-tuple-element.21), channel_id=1, source_target_pairs={{0,1},{1,2},{2,3},{3,4},{4,5},{5,6},{6,7},{8,9},{9,10},{10,11},{11... | collective-permute-start | bytes 1572872 | tf_op jit(solution)/shard_map/ppermute | solution.py:16
  84.3 21.5 %collective-permute-start.3 = (f32[16,8,1024]{2,1,0:T(8,128)S(1)}, f32[16,8,1024]{2,1,0:T(8,128)S(1)}, u32[]{:S(2)}, u32[]{:S(2)}) collective-permute-start(f32[16,8,1024]{2,1,0:T(8,128)S(1)} %get-tuple-element.21), channel_id=1, source_target_pairs={{1,0},{2,1},{3,2},{4,3},{5,4},{6,5},{7,6},{9,8},{10,9},{11,10},{12... | collective-permute-start | bytes 1572872 | tf_op jit(solution)/shard_map/ppermute | solution.py:19
  122.7 6.2 %copy-start = (bf16[16,16,2048]{2,1,0:T(8,128)(2,1)S(1)}, bf16[16,16,2048]{2,1,0:T(8,128)(2,1)}, u32[]{:S(2)}) copy-start(bf16[16,16,2048]{2,1,0:T(8,128)(2,1)} %param.5) | copy-start | bytes 3145732
  130.7 21.9 %copy-start.2 = (f32[1,2048]{1,0:T(1,128)S(1)}, f32[1,2048]{1,0:T(1,128)}, u32[]{:S(2)}) copy-start(f32[1,2048]{1,0:T(1,128)} %param.9) | copy-start | bytes 24580
  130.8 21.9 %copy-start.3 = (f32[1,2048]{1,0:T(1,128)S(1)}, f32[1,2048]{1,0:T(1,128)}, u32[]{:S(2)}) copy-start(f32[1,2048]{1,0:T(1,128)} %param.8) | copy-start | bytes 24580
  152.7 67.2 %copy-start.5 = (f32[2048]{0:T(1024)}, f32[2048]{0:T(1024)S(1)}, u32[]{:S(2)}) copy-start(f32[2048]{0:T(1024)S(1)} %reduce_sum.138) | copy-start | bytes 24580
  241.9 26.1 %collective-permute-start.4 = (f32[16,8,1024]{2,1,0:T(8,128)S(1)}, f32[16,8,1024]{2,1,0:T(8,128)S(1)}, u32[]{:S(2)}, u32[]{:S(2)}) collective-permute-start(f32[16,8,1024]{2,1,0:T(8,128)S(1)} %fusion.10), channel_id=1, source_target_pairs={{0,1},{1,2},{2,3},{3,4},{4,5},{5,6},{6,7},{8,9},{9,10},{10,11},{11... | collective-permute-start | bytes 1572872 | tf_op jit(solution)/shard_map/ppermute | solution.py:16
  246.4 21.6 %collective-permute-start.5 = (f32[16,8,1024]{2,1,0:T(8,128)S(1)}, f32[16,8,1024]{2,1,0:T(8,128)S(1)}, u32[]{:S(2)}, u32[]{:S(2)}) collective-permute-start(f32[16,8,1024]{2,1,0:T(8,128)S(1)} %fusion.10), channel_id=1, source_target_pairs={{1,0},{2,1},{3,2},{4,3},{5,4},{6,5},{7,6},{9,8},{10,9},{11,10},{12... | collective-permute-start | bytes 1572872 | tf_op jit(solution)/shard_map/ppermute | solution.py:19
  269.6 25.2 %collective-permute-start.6 = (f32[16,8,1024]{2,1,0:T(8,128)S(1)}, f32[16,8,1024]{2,1,0:T(8,128)S(1)}, u32[]{:S(2)}, u32[]{:S(2)}) collective-permute-start(f32[16,8,1024]{2,1,0:T(8,128)S(1)} %get-tuple-element.19), channel_id=1, source_target_pairs={{0,1},{1,2},{2,3},{3,4},{4,5},{5,6},{6,7},{8,9},{9,10},{10,11},{11... | collective-permute-start | bytes 1572872 | tf_op jit(solution)/shard_map/ppermute | solution.py:16
  274.1 20.7 %collective-permute-start.7 = (f32[16,8,1024]{2,1,0:T(8,128)S(1)}, f32[16,8,1024]{2,1,0:T(8,128)S(1)}, u32[]{:S(2)}, u32[]{:S(2)}) collective-permute-start(f32[16,8,1024]{2,1,0:T(8,128)S(1)} %get-tuple-element.19), channel_id=1, source_target_pairs={{1,0},{2,1},{3,2},{4,3},{5,4},{6,5},{7,6},{9,8},{10,9},{11,10},{12... | collective-permute-start | bytes 1572872 | tf_op jit(solution)/shard_map/ppermute | solution.py:19
  319.7 21.9 %copy-start.4 = (f32[1,2048]{1,0:T(1,128)S(1)}, f32[1,2048]{1,0:T(1,128)}, u32[]{:S(2)}) copy-start(f32[1,2048]{1,0:T(1,128)} %param.8) | copy-start | bytes 24580
  319.7 21.9 %copy-start.6 = (f32[2048]{0:T(1024)S(1)}, f32[2048]{0:T(1024)}, u32[]{:S(2)}) copy-start(f32[2048]{0:T(1024)} %copy-done.5) | copy-start | bytes 24580
  428.5 31.3 %copy-start.8 = (f32[8,24]{1,0:T(8,128)S(1)}, f32[8,24]{1,0:T(8,128)}, u32[]{:S(2)}) copy-start(f32[8,24]{1,0:T(8,128)} %copy-done.7) | copy-start | bytes 2308
  433.5 26.3 %collective-permute-start.8 = (f32[16,8,1024]{2,1,0:T(8,128)S(1)}, f32[16,8,1024]{2,1,0:T(8,128)S(1)}, u32[]{:S(2)}, u32[]{:S(2)}) collective-permute-start(f32[16,8,1024]{2,1,0:T(8,128)S(1)} %fusion.6), channel_id=1, source_target_pairs={{0,1},{1,2},{2,3},{3,4},{4,5},{5,6},{6,7},{8,9},{9,10},{10,11},{11... | collective-permute-start | bytes 1572872 | tf_op jit(solution)/shard_map/ppermute | solution.py:16
  438.0 21.8 %collective-permute-start.9 = (f32[16,8,1024]{2,1,0:T(8,128)S(1)}, f32[16,8,1024]{2,1,0:T(8,128)S(1)}, u32[]{:S(2)}, u32[]{:S(2)}) collective-permute-start(f32[16,8,1024]{2,1,0:T(8,128)S(1)} %fusion.6), channel_id=1, source_target_pairs={{1,0},{2,1},{3,2},{4,3},{5,4},{6,5},{7,6},{9,8},{10,9},{11,10},{12... | collective-permute-start | bytes 1572872 | tf_op jit(solution)/shard_map/ppermute | solution.py:19
  462.2 25.3 %collective-permute-start.10 = (f32[16,8,1024]{2,1,0:T(8,128)S(1)}, f32[16,8,1024]{2,1,0:T(8,128)S(1)}, u32[]{:S(2)}, u32[]{:S(2)}) collective-permute-start(f32[16,8,1024]{2,1,0:T(8,128)S(1)} %get-tuple-element.16), channel_id=1, source_target_pairs={{0,1},{1,2},{2,3},{3,4},{4,5},{5,6},{6,7},{8,9},{9,10},{10,11},{11... | collective-permute-start | bytes 1572872 | tf_op jit(solution)/shard_map/ppermute | solution.py:16
  466.6 20.9 %collective-permute-start.11 = (f32[16,8,1024]{2,1,0:T(8,128)S(1)}, f32[16,8,1024]{2,1,0:T(8,128)}, u32[]{:S(2)}, u32[]{:S(2)}) collective-permute-start(f32[16,8,1024]{2,1,0:T(8,128)S(1)} %get-tuple-element.16), channel_id=1, source_target_pairs={{1,0},{2,1},{3,2},{4,3},{5,4},{6,5},{7,6},{9,8},{10,9},{11,10},{12... | collective-permute-start | bytes 1572872 | tf_op jit(solution)/shard_map/ppermute | solution.py:19
  513.7 21.9 %copy-start.9 = (f32[2048]{0:T(1024)S(1)}, f32[2048]{0:T(1024)}, u32[]{:S(2)}) copy-start(f32[2048]{0:T(1024)} %get-tuple-element.9) | copy-start | bytes 24580
  513.7 68.1 %copy-start.1 = (f32[16,8,1024]{2,1,0:T(8,128)S(1)}, f32[16,8,1024]{2,1,0:T(8,128)}, u32[]{:S(2)}) copy-start(f32[16,8,1024]{2,1,0:T(8,128)} %get-tuple-element.42) | copy-start | bytes 1572868
Sparse Core Ops, SparseCore 0:
  581.9 20.8 reduce-scatter.1
